TPU v7x, 512 devices: a whole 4x4x16 slice. The times are simulated.
512 devices in a mesh: ep: 128 (over x, z, core), dp: 4 (over y).
Axes of the slice: x: 4, y: 4, z: 16, core: 2. Of those that a mesh axis runs over, the one named last changes fastest.
Arguments:
- tokens: bfloat16 [2048, 3584], P('ep'), may hold values from -6 to 6
- expert_ids: int32 [2048, 8], P('ep'), may hold values from 0 to 127, all different within a row; in each aligned block of 16 rows (0 to 15, 16 to 31, ...) at most 4 rows name the same one
- route_logits: float32 [2048, 8], P('ep'), may hold values from -8 to 8
- expert_gate: bfloat16 [128, 3584, 1024], P('ep', None, 'dp'), may hold values from -0.09375 to 0.09375
- expert_up: bfloat16 [128, 3584, 1024], P('ep', None, 'dp'), may hold values from -0.09375 to 0.09375
- expert_down: bfloat16 [128, 1024, 3584], P('ep', 'dp'), may hold values from -0.1875 to 0.1875
Outputs:
- mixed: bfloat16 [2048, 3584], P(('ep', 'dp'))
Inputs may be any that keep to these rules, and one draw needn't show every extreme that they name: `expert_ids`: each row names 8 different experts of 0 to 127 and every expert is named by some row. Within the rows of one index of ep (aligned blocks of 16 rows) no expert is named more than 4 times, and some block names one expert exactly 4 times. Loads are heavy-tailed: a few experts take several times the mean.
All inputs are finite; a program needn't handle non-finite values.
Results may differ from a plain program's by a relative error of at most 0.015.
Values may be sent and summed in bfloat16 or wider, within the bound.
A program may use at most 64 MiB of HBM per device.

v0:
```python
import jax
import jax.numpy as jnp
from jax import lax
from jax.sharding import PartitionSpec as P

route_scale = 2.5


def on_device(tokens, expert_ids, route_logits, expert_gate, expert_up, expert_down):
    tok_rows, width = tokens.shape
    top = expert_ids.shape[1]
    n_ep = lax.axis_size("ep")
    n_dp = lax.axis_size("dp")
    experts = n_ep
    capacity = min(tok_rows, 4 * max(1, tok_rows * top // experts))
    flat_ids = expert_ids.reshape(-1).astype(jnp.int32)
    onehot = (flat_ids[:, None] == jnp.arange(experts, dtype=jnp.int32)[None, :]).astype(jnp.int32)
    earlier = jnp.cumsum(onehot, axis=0).astype(jnp.int32) - onehot
    within = jnp.sum(earlier * onehot, axis=1).astype(jnp.int32)
    slot_index = flat_ids * capacity + within
    token_of_slot = jnp.arange(tok_rows * top, dtype=jnp.int32) // top
    source_row = (
        jnp.full((experts * capacity,), tok_rows, jnp.int32).at[slot_index].set(token_of_slot)
    )
    extended = jnp.concatenate([tokens, jnp.zeros((1, width), tokens.dtype)], axis=0)
    outgoing = extended[source_row].reshape(n_ep, capacity, width)
    arrived = lax.all_to_all(outgoing, "ep", split_axis=0, concat_axis=0, tiled=True)
    received = arrived.reshape(n_ep * capacity, width)
    gate = jnp.dot(received, expert_gate[0], preferred_element_type=jnp.float32)
    upper = jnp.dot(received, expert_up[0], preferred_element_type=jnp.float32)
    hidden = (jax.nn.silu(gate) * upper).astype(jnp.bfloat16)
    partial_value = jnp.dot(hidden, expert_down[0], preferred_element_type=jnp.float32)
    partial_value = partial_value.reshape(n_ep, capacity, width)
    scores = jax.nn.sigmoid(route_logits)
    weights = route_scale * scores / jnp.sum(scores, axis=1, keepdims=True)
    member = lax.axis_index("dp")
    quarter = capacity // n_dp
    reduced = (
        lax.psum_scatter(partial_value.astype(jnp.bfloat16), "dp", scatter_dimension=1, tiled=True)
        .astype(jnp.float32)
        .astype(jnp.bfloat16)
    )
    back = lax.all_to_all(reduced, "ep", split_axis=0, concat_axis=0, tiled=True)
    offset = within - member * quarter
    held = ((offset >= 0) & (offset < quarter)).astype(jnp.float32)
    picked = flat_ids * quarter + jnp.clip(offset, 0, quarter - 1)
    values = back.reshape(experts * quarter, width)[picked].reshape(tok_rows, top, width)
    masked = weights * held.reshape(tok_rows, top)
    contrib = jnp.sum(masked[:, :, None] * values.astype(jnp.float32), axis=1)
    routed = lax.psum_scatter(
        contrib.astype(jnp.bfloat16), "dp", scatter_dimension=0, tiled=True
    ).astype(jnp.float32)
    return routed.astype(jnp.bfloat16)


def solution(mesh):
    placed = (
        P("ep", None),
        P("ep", None),
        P("ep", None),
        P("ep", None, "dp"),
        P("ep", None, "dp"),
        P("ep", "dp", None),
    )
    return jax.shard_map(
        on_device, mesh=mesh, in_specs=placed, out_specs=P(("ep", "dp"), None), check_vma=False
    )
```

profile of v0, /device:TPU:1, one launch (start us, length us, event | category | flops | bytes accessed | tf_op | source)
XLA Modules:
  0.0 400.9 jit_solution(13666367632085230634)
XLA Ops:
  6.5 0.0 copy-start
  6.5 0.0 reduce-scatter.2.cloned.1.call-start
  6.5 0.9 copy.20
  7.4 0.1 eq.15
  7.5 0.1 reshape.87
  7.6 0.1 fusion.13
  7.7 0.2 reduce_window_sum.11
  7.9 0.2 select_reduce_fusion
  8.1 1.0 scatter_custom_fusion
  9.1 0.9 concatenate.3
  10.0 4.2 %gather_fusion = bf16[512,3584]{1,0:T(8,128)(2,1)} fusion(bf16[17,3584]{1,0:T(8,128)(2,1)S(1)} %concatenate.3, s32[1024]{0:T(1024)S(1)} %pad_clamp_fusion.1), kind=kCustom, calls=%fused_computation | custom fusion | bytes 7342080 | tf_op jit(solution)/shard_map/gather | solution.py:26
  14.2 7.0 %reshape.88 = bf16[128,4,3584]{2,1,0:T(4,128)(2,1)} reshape(bf16[512,3584]{1,0:T(8,128)(2,1)} %gather_fusion) | data formatting | bytes 7340032 | tf_op jit(solution)/shard_map/reshape | solution.py:26
  21.2 190.3 %all_to_all.10 = bf16[128,4,3584]{2,1,0:T(4,128)(2,1)} all-to-all(bf16[128,4,3584]{2,1,0:T(4,128)(2,1)} %reshape.88), channel_id=1, replica_groups=mesh['ep'=128,'dp'=4] {'ep'}, dimensions={0} | all-to-all | bytes 7340032 | tf_op jit(solution)/shard_map/all_to_all | solution.py:27
  211.5 6.7 %reshape.89 = bf16[512,3584]{1,0:T(8,128)(2,1)} reshape(bf16[128,4,3584]{2,1,0:T(4,128)(2,1)} %all_to_all.10) | data formatting | bytes 7340032 | tf_op jit(solution)/shard_map/reshape | solution.py:28
  218.2 0.0 copy-start.1
  218.2 0.0 copy-start.3
  218.2 3.9 fusion.4
  222.1 0.0 copy-done.1
  222.1 0.4 copy-done.3
  222.5 1.1 fusion.9
  223.6 0.1 dot_general.13
  223.7 0.0 copy-done
  223.7 2.9 convolution_convert_fusion
  226.6 0.0 reduce-scatter.2.cloned.1.call-update
  226.6 0.0 copy-start.2
  226.6 41.8 %reduce-scatter.2.cloned.1.call-done = bf16[128,1,3584]{2,0,1:T(8,128)(2,1)} async-done(((bf16[128,4,3584]{2,0,1:T(8,128)(2,1)}), bf16[128,1,3584]{2,0,1:T(8,128)(2,1)}) %reduce-scatter.2.cloned.1.call-update) | async-done | bytes 917520 | tf_op jit(solution)/shard_map/reduce_scatter | solution.py:39
  268.4 0.5 broadcast.120
  268.9 2.5 reduce
  271.4 1.1 reshape.121
  272.6 16.9 %all-to-all-start.1 = ((bf16[128,2,1792]{2,1,0:T(2,128)(2,1)}), bf16[128,2,1792]{2,1,0:T(2,128)(2,1)S(1)}, u32[]{:S(2)}, u32[]{:S(2)}) async-start(bf16[128,2,1792]{2,1,0:T(2,128)(2,1)} %reshape.121), calls=%async_computation.2 | async-start | bytes 1835008 | tf_op jit(solution)/shard_map/all_to_all | solution.py:43
  289.5 0.0 all-reduce.4.cloned.1.call-start
  289.5 0.1 and.14
  289.6 0.0 copy-done.2
  289.6 0.1 copy.21
  289.7 0.1 fusion.14
  289.8 0.1 divide_select_fusion
  289.9 49.9 %all-to-all-done.1 = bf16[128,2,1792]{2,1,0:T(2,128)(2,1)S(1)} async-done(((bf16[128,2,1792]{2,1,0:T(2,128)(2,1)}), bf16[128,2,1792]{2,1,0:T(2,128)(2,1)S(1)}, u32[]{:S(2)}, u32[]{:S(2)}) %all-to-all-start.1) | async-done | bytes 917536 | tf_op jit(solution)/shard_map/all_to_all | solution.py:43
  339.8 2.1 reshape.122
  341.9 1.6 copy.29
  343.5 2.1 gather_fusion.1
  345.6 2.5 fusion
  348.1 0.0 all-reduce.4.cloned.1.call-update
  348.1 1.3 dynamic-slice
  350.1 42.6 %all-reduce.4.cloned.1.call-done = bf16[16,3584]{1,0:T(8,128)(2,1)} async-done(((bf16[16,3584]{1,0:T(8,128)(2,1)}), bf16[16,3584]{1,0:T(8,128)(2,1)}) %all-reduce.4.cloned.1.call-update) | async-done | bytes 114704
  392.6 1.4 constant_dynamic-slice_fusion
  (6 shorter events, 0.0 us)
Async XLA Ops:
  6.5 217.1 %copy-start = (bf16[1,256,3584]{2,1,0:T(8,128)(2,1)S(1)}, bf16[1,256,3584]{2,1,0:T(8,128)(2,1)}, u32[]{:S(2)}) copy-start(bf16[1,256,3584]{2,1,0:T(8,128)(2,1)} %param.11) | copy-start | bytes 5505028
  6.5 261.9 %reduce-scatter.2.cloned.1.call-start = ((), (), s32[]{:S(2)}) async-start(), calls=%async_computation.3 | async-start | bytes 4587520 | tf_op jit(solution)/shard_map/reduce_scatter | solution.py:39
  218.2 3.9 copy-start.1
  218.2 4.3 %copy-start.3 = (bf16[1,3584,256]{2,1,0:T(8,128)(2,1)S(1)}, bf16[1,3584,256]{2,1,0:T(8,128)(2,1)}, u32[]{:S(2)}) copy-start(bf16[1,3584,256]{2,1,0:T(8,128)(2,1)} %param.10) | copy-start | bytes 5505028
  226.6 63.0 %copy-start.2 = (f32[16,8]{0,1:T(8,128)S(1)}, f32[16,8]{0,1:T(8,128)}, u32[]{:S(2)}) copy-start(f32[16,8]{0,1:T(8,128)} %param.8) | copy-start | bytes 1540
  272.6 67.2 %all-to-all-start.1 = ((bf16[128,2,1792]{2,1,0:T(2,128)(2,1)}), bf16[128,2,1792]{2,1,0:T(2,128)(2,1)S(1)}, u32[]{:S(2)}, u32[]{:S(2)}) async-start(bf16[128,2,1792]{2,1,0:T(2,128)(2,1)} %reshape.121), calls=%async_computation.2 | async-start | bytes 1835008 | tf_op jit(solution)/shard_map/all_to_all | solution.py:43
  289.5 103.2 %all-reduce.4.cloned.1.call-start = ((), (), s32[]{:S(2)}) async-start(), calls=%async_computation.4 | async-start | bytes 229376
Sparse Core Ops, SparseCore 0:
  226.7 41.6 reduce-scatter.1
  348.3 44.3 all-reduce.3
where the time goes:
time: 403 us; the launch traced here: 401 us
  blocking collectives  190 us (47%)
  waiting for transfers between devices  134 us (33%)
  local copies, waits for them, and re-layouts  31.7 us (8%)
  starting transfers between devices  16.9 us (4%)
  between operations  14.2 us (4%)
  matrix products  7.88 us (2%)
  other arithmetic  5.68 us (1%)
    all_to_all x1, blocking collectives, on_device(): lax.all_to_all(outgoing, 'ep', split_axis=0, concat_axis=0, tiled=True)  190 us
    all_to_all x1, waiting for transfers between devices, on_device(): lax.all_to_all(reduced, 'ep', split_axis=0, concat_axis=0, tiled=True)  49.9 us
    unnamed x3, waiting for transfers between devices  42.6 us
    reduce_scatter x1, waiting for transfers between devices, on_device(): lax.psum_scatter(partial_value.astype(jnp.bfloat16), 'dp', scatter_dimens...  41.8 us
    all_to_all x1, starting transfers between devices, on_device(): lax.all_to_all(reduced, 'ep', split_axis=0, concat_axis=0, tiled=True)  16.9 us
    unnamed x15, local copies, waits for them, and re-layouts  8.92 us
  transfers between devices with their start and end apart: 3, of which 3 were waited for; matrix products, arithmetic and copies ran while one was open for 0% of the time, Pallas kernels for 0%

commit v1 on v0

v1 whole, which is shorter than its diff:
```python
import functools

import jax
import jax.numpy as jnp
from jax import lax
from jax.experimental import pallas as pl
from jax.experimental.pallas import tpu as pltpu
from jax.sharding import PartitionSpec as P

route_scale = 2.5
MESH = pl.DeviceIdType.MESH
NX = 4
NZ = 16
ROWS = 16
HALF = NZ // 2
NEAR = HALF - 1
LANES = 128
ZA_GATHER = 11 * LANES
ZA_SCATTER = 10 * LANES
f32 = jnp.float32
bf16 = jnp.bfloat16


def place():
    ep = lax.axis_index("ep")
    y = lax.axis_index("dp")
    core = lax.rem(ep, 2)
    z = lax.rem(ep // 2, NZ)
    x = ep // (2 * NZ)

    def dev(x_, z_, core_):
        return ((lax.rem(x_ + NX, NX) * NZ + lax.rem(z_ + NZ, NZ)) * 2 + core_, y)

    return ep, x, y, z, core, dev


def remote(src, dst, send, recv, device):
    return pltpu.make_async_remote_copy(
        src_ref=src, dst_ref=dst, send_sem=send, recv_sem=recv, device_id=device, device_id_type=MESH
    )


def greet(peers):
    barrier = pltpu.get_barrier_semaphore()
    for device in peers:
        pl.semaphore_signal(barrier, inc=1, device_id=device, device_id_type=MESH)
    return barrier


def within(k, low, high):
    return jnp.logical_and(k >= low, k <= high)


def gather_kernel(
    tok, ids, logits, wg_hbm, wu_hbm, hid,
    ga, gb, wg, wu, wsem, ax_s, ax_r, za_s, za_r, zb_s, zb_r, xb_s, xb_r, ca_s, ca_r, cb_s, cb_r,
):
    ep, x, y, z, core, dev = place()
    fa = ga.shape[-1]
    fb = gb.shape[-1] - LANES
    other = 1 - core
    barrier = greet(
        [dev(x + 1, z, core), dev(x + 3, z, core), dev(x + 2, z, core), dev(x, z + 1, core), dev(x, z + 15, core), dev(x, z, other)]
    )
    copy_g = pltpu.make_async_copy(wg_hbm.at[0], wg, wsem.at[0])
    copy_u = pltpu.make_async_copy(wu_hbm.at[0], wu, wsem.at[1])
    copy_g.start()
    copy_u.start()

    ga[z, 0, x] = tok[:, :fa]
    gb[z, 0, x, :, :fb] = tok[:, fa:]
    scores = jax.nn.sigmoid(logits[...])
    weights = route_scale * scores / jnp.sum(scores, axis=1, keepdims=True)
    names = ids[...]
    lane = lax.broadcasted_iota(jnp.int32, (ROWS, LANES), 1)
    table = jnp.zeros((ROWS, LANES), f32)
    for k in range(8):
        table = table + jnp.where(names[:, k : k + 1] == lane, weights[:, k : k + 1], 0.0)
    gb[z, 0, x, :, fb:] = table.astype(bf16)
    pl.semaphore_wait(barrier, 6)

    def zdev(s):
        return dev(x, z + 1, core) if s == 0 else dev(x, z + 15, core)

    def at(s, k):
        return lax.rem(z + NZ - k, NZ) if s == 0 else lax.rem(z + k, NZ)

    def ax(j):
        return remote(ga.at[z, 0, x], ga.at[z, 0, x], ax_s.at[j], ax_r.at[j], dev(x + j + 1, z, core))

    def za(s, h, k, d):
        ref = ga.at[d, 0, pl.ds(2 * h, 2)]
        return remote(ref, ref, za_s.at[s, h, k], za_r.at[s, h, k], zdev(s))

    def zb(s, k, d):
        ref = gb.at[d, 0, x]
        return remote(ref, ref, zb_s.at[s, k], zb_r.at[s, k], zdev(s))

    def xb(d, j, row, step):
        ref = gb.at[d, 0, lax.rem(row + NX, NX)]
        return remote(ref, ref, xb_s.at[d, j], xb_r.at[d, j], dev(x + step, z, core))

    def ca(d):
        return remote(ga.at[d, 0], ga.at[d, 1], ca_s.at[d], ca_r.at[d], dev(x, z, other))

    def cb(d):
        return remote(gb.at[d, 0], gb.at[d, 1], cb_s.at[d], cb_r.at[d], dev(x, z, other))

    for j in range(3):
        ax(j).start()
    for s in range(2):
        zb(s, 1, z).start()
    xb(z, 0, x, 1).start()
    xb(z, 1, x, 3).start()
    for j in range(3):
        ax(j).wait_recv()
    for h in range(2):
        for s in range(2):
            za(s, h, 1, z).start()
    copy_g.wait()
    copy_u.wait()

    def mine(s, k):
        return within(k, 0, NEAR) if s == 0 else within(k, 1, HALF)

    def compute(d):
        ca(d).wait_recv()
        cb(d).wait_recv()
        rows_a = ga[d].reshape(2 * NX * ROWS, fa)
        rows_b = gb[d, :, :, :, :fb].reshape(2 * NX * ROWS, fb)
        side = gb[d, :, :, :, fb:].reshape(2 * NX * ROWS, LANES).astype(f32)
        here = lax.broadcasted_iota(jnp.int32, side.shape, 1) == ep
        scale = jnp.sum(jnp.where(here, side, 0.0), axis=1, keepdims=True)
        gate = jnp.dot(rows_a, wg[:fa, :], preferred_element_type=f32) + jnp.dot(rows_b, wg[fa:, :], preferred_element_type=f32)
        upper = jnp.dot(rows_a, wu[:fa, :], preferred_element_type=f32) + jnp.dot(rows_b, wu[fa:, :], preferred_element_type=f32)
        hidden = gate / (1.0 + jnp.exp(-gate)) * upper * scale
        hid[d] = hidden.astype(bf16).reshape(2, NX, ROWS, hidden.shape[-1])

    def step(k, carry):
        for s in range(2):
            top = NEAR if s == 0 else HALF

            @pl.when(within(k, 1, top))
            def _():
                d = at(s, k)
                zb(s, k, d).wait_recv()

                @pl.when(k < top)
                def _():
                    zb(s, k + 1, d).start()

                xb(d, 0, x, 1).start()
                xb(d, 1, x, 3).start()

        for h in range(2):
            for s in range(2):
                top = HALF if s == h else NEAR

                @pl.when(within(k, 1, top))
                def _():
                    d = at(s, k)
                    za(s, h, k, d).wait_recv()

                    @pl.when(k < top)
                    def _():
                        za(s, h, k + 1, d).start()

        for s in range(2):

            @pl.when(mine(s, k))
            def _():
                ca(at(s, k)).start()

        for s in range(2):

            @pl.when(mine(s, k - 1))
            def _():
                d = at(s, k - 1)
                xb(d, 0, x + 3, 1).wait_recv()
                xb(d, 1, x + 1, 1).wait_recv()
                if s == 0:
                    xb(d, 2, x + 3, 1).start()
                else:
                    xb(d, 2, x + 1, 3).start()

        for s in range(2):

            @pl.when(mine(s, k - 2))
            def _():
                d = at(s, k - 2)
                xb(d, 2, x + 2, 1).wait_recv()
                cb(d).start()

        for s in range(2):

            @pl.when(mine(s, k - 3))
            def _():
                compute(at(s, k - 3))

        return carry

    lax.fori_loop(0, HALF + 4, step, 0)

    for j in range(3):
        ax(j).wait_send()

    def drain(k, carry):
        for s in range(2):
            top = NEAR if s == 0 else HALF

            @pl.when(k <= top)
            def _():
                zb(s, k, z).wait_send()

        for h in range(2):
            for s in range(2):
                top = HALF if s == h else NEAR

                @pl.when(k <= top)
                def _():
                    za(s, h, k, z).wait_send()

        return carry

    lax.fori_loop(1, HALF + 1, drain, 0)

    def drain_all(d, carry):
        for j in range(3):
            xb(d, j, x, 1).wait_send()
        ca(d).wait_send()
        cb(d).wait_send()
        return carry

    lax.fori_loop(0, NZ, drain_all, 0)


def scatter_kernel(
    hid, wd_hbm, out,
    wd, own, sib_out, sib_in, a_out, a_in, b_out, b_in, x_out, x_in, f_out, f_in, y_out, y_in,
    wsem, c_s, c_r, a_s, a_r, b_s, b_r, x_s, x_r, f_s, f_r, y_s, y_r,
):
    ep, x, y, z, core, dev = place()
    width = own.shape[-1]
    fa = a_out.shape[-1]
    fb = width - fa
    other = 1 - core
    n_dp = y_out.shape[0]

    def ydev(j):
        return (ep, lax.rem(y + j, n_dp))

    barrier = greet(
        [dev(x + 1, z, core), dev(x + 3, z, core), dev(x + 2, z, core), dev(x, z + 1, core), dev(x, z + 15, core), dev(x, z, other)]
        + [ydev(j) for j in range(1, n_dp)]
    )
    copy_d = pltpu.make_async_copy(wd_hbm.at[0], wd, wsem)
    copy_d.start()
    pl.semaphore_wait(barrier, 6 + n_dp - 1)
    copy_d.wait()

    def at(s, k):
        return lax.rem(z + k, NZ) if s == 0 else lax.rem(z + NZ - k, NZ)

    def zdev(s):
        return dev(x, z + 1, core) if s == 0 else dev(x, z + 15, core)

    def xmod(v):
        return lax.rem(v + NX, NX)

    def cc(d):
        return remote(sib_out.at[d], sib_in.at[d], c_s.at[d], c_r.at[d], dev(x, z, other))

    def ra(s, h, k):
        return remote(a_out.at[s, h, k], a_in.at[s, h, k], a_s.at[s, h, k], a_r.at[s, h, k], zdev(s))

    def rb(s, k):
        return remote(b_out.at[s, k], b_in.at[s, k], b_s.at[s, k], b_r.at[s, k], zdev(s))

    def rx(d, j, step):
        return remote(x_out.at[d, j], x_in.at[d, j], x_s.at[d, j], x_r.at[d, j], dev(x + step, z, core))

    def rf(j):
        return remote(f_out.at[j], f_in.at[j], f_s.at[j], f_r.at[j], dev(x + j + 1, z, core))

    def ry(j):
        return remote(y_out.at[lax.rem(y + j, n_dp)], y_in.at[j], y_s.at[j], y_r.at[j], ydev(j))

    def term_a(d, h):
        rows = pl.ds(2 * h, 2)
        return own[d, rows, :, :fa].astype(f32) + sib_in[d, rows, :, :fa].astype(f32)

    def term_b(d, row):
        return own[d, row, :, fa:].astype(f32) + sib_in[d, row, :, fa:].astype(f32)

    def project(d):
        rows = hid[d].reshape(2 * NX * ROWS, hid.shape[-1])
        cut = 512

        def piece(n, carry):
            columns = pl.ds(pl.multiple_of(n * cut, cut), cut)
            value = jnp.dot(rows, wd[:, columns], preferred_element_type=f32).astype(bf16)
            value = value.reshape(2, NX, ROWS, cut)
            own[d, :, :, columns] = value[0]
            sib_out[d, :, :, columns] = value[1]
            return carry

        lax.fori_loop(0, width // cut, piece, 0)
        cc(d).start()

    def has(s, k):
        return within(k, 0, NEAR) if s == 0 else within(k, 1, HALF)

    def step(t, carry):
        k0 = HALF - t
        for s in range(2):

            @pl.when(has(s, k0))
            def _():
                project(at(s, k0))

        k1 = HALF + 1 - t
        for s in range(2):

            @pl.when(has(s, k1))
            def _():
                cc(at(s, k1)).wait_recv()

        for h in range(2):
            for s in range(2):
                top = HALF if s == h else NEAR

                @pl.when(k1 == top)
                def _():
                    d = at(s, k1)
                    a_out[s, h, k1] = term_a(d, h).astype(bf16)
                    ra(s, h, k1).start()

                @pl.when(within(k1, 1, top - 1))
                def _():
                    d = at(s, k1)
                    ra(s, h, k1 + 1).wait_recv()
                    a_out[s, h, k1] = (term_a(d, h) + a_in[s, h, k1 + 1].astype(f32)).astype(bf16)
                    ra(s, h, k1).start()

        for s in range(2):
            go, back = (1, 3) if s == 0 else (3, 1)

            @pl.when(has(s, k1))
            def _():
                d = at(s, k1)
                x_out[d, 0] = term_b(d, xmod(x + 2)).astype(bf16)
                rx(d, 0, go).start()
                x_out[d, 1] = term_b(d, xmod(x + back)).astype(bf16)
                rx(d, 1, back).start()

        k2 = HALF + 2 - t
        for s in range(2):
            go, back = (1, 3) if s == 0 else (3, 1)

            @pl.when(has(s, k2))
            def _():
                d = at(s, k2)
                rx(d, 0, go).wait_recv()
                x_out[d, 2] = (term_b(d, xmod(x + go)) + x_in[d, 0].astype(f32)).astype(bf16)
                rx(d, 2, go).start()

        k3 = HALF + 3 - t
        for s in range(2):
            top = NEAR if s == 0 else HALF

            @pl.when(jnp.logical_and(has(s, k3), k3 >= 1))
            def _():
                d = at(s, k3)
                rx(d, 1, 1).wait_recv()
                rx(d, 2, 1).wait_recv()
                total = term_b(d, x) + x_in[d, 1].astype(f32) + x_in[d, 2].astype(f32)

                @pl.when(k3 == top)
                def _():
                    b_out[s, k3] = total.astype(bf16)

                @pl.when(k3 < top)
                def _():
                    rb(s, k3 + 1).wait_recv()
                    b_out[s, k3] = (total + b_in[s, k3 + 1].astype(f32)).astype(bf16)

                rb(s, k3).start()

        return carry

    lax.fori_loop(0, HALF + 3, step, 0)

    for h in range(2):
        for s in range(2):
            ra(s, h, 1).wait_recv()
    for j in range(3):
        row = xmod(x + j + 1)
        sums = own[z, row, :, :fa].astype(f32) + sib_in[z, row, :, :fa].astype(f32)
        sums = sums + a_in[0, row // 2, 1, lax.rem(row, 2)].astype(f32) + a_in[1, row // 2, 1, lax.rem(row, 2)].astype(f32)
        f_out[j] = sums.astype(bf16)
        rf(j).start()
    total_a = own[z, x, :, :fa].astype(f32) + sib_in[z, x, :, :fa].astype(f32)
    total_a = total_a + a_in[0, x // 2, 1, lax.rem(x, 2)].astype(f32) + a_in[1, x // 2, 1, lax.rem(x, 2)].astype(f32)

    rx(z, 1, 1).wait_recv()
    rx(z, 2, 1).wait_recv()
    total_b = term_b(z, x) + x_in[z, 1].astype(f32) + x_in[z, 2].astype(f32)
    for s in range(2):
        rb(s, 1).wait_recv()
        total_b = total_b + b_in[s, 1].astype(f32)
    for j in range(3):
        rf(j).wait_recv()
        total_a = total_a + f_in[j].astype(f32)
    part = ROWS // n_dp
    for j in range(n_dp):
        y_out[j, :, :fa] = total_a[part * j : part * (j + 1)]
        y_out[j, :, fa:] = total_b[part * j : part * (j + 1)]
    for j in range(1, n_dp):
        ry(j).start()
    result = y_out[y]
    for j in range(1, n_dp):
        ry(j).wait_recv()
        result = result + y_in[j]
    out[...] = result.astype(bf16)

    for j in range(1, n_dp):
        ry(j).wait_send()
    for j in range(3):
        rf(j).wait_send()

    def drain(k, carry):
        for s in range(2):
            top = NEAR if s == 0 else HALF

            @pl.when(k <= top)
            def _():
                rb(s, k).wait_send()

        for h in range(2):
            for s in range(2):
                top = HALF if s == h else NEAR

                @pl.when(k <= top)
                def _():
                    ra(s, h, k).wait_send()

        return carry

    lax.fori_loop(1, HALF + 1, drain, 0)

    def drain_all(d, carry):
        for j in range(3):
            rx(d, j, 1).wait_send()
        cc(d).wait_send()
        return carry

    lax.fori_loop(0, NZ, drain_all, 0)


def on_device(tokens, expert_ids, route_logits, expert_gate, expert_up, expert_down):
    width = tokens.shape[1]
    n_dp = lax.axis_size("dp")
    cut = expert_gate.shape[2]
    vmem = pl.BlockSpec(memory_space=pltpu.VMEM)
    whole = pl.BlockSpec(memory_space=pl.ANY)
    dma = pltpu.SemaphoreType.DMA
    fa, fb = ZA_GATHER, width - ZA_GATHER
    hidden = pl.pallas_call(
        gather_kernel,
        name="gather_up",
        out_shape=jax.ShapeDtypeStruct((NZ, 2, NX, ROWS, cut), bf16),
        in_specs=[vmem, vmem, vmem, whole, whole],
        out_specs=vmem,
        scratch_shapes=[
            pltpu.VMEM((NZ, 2, NX, ROWS, fa), bf16),
            pltpu.VMEM((NZ, 2, NX, ROWS, fb + LANES), bf16),
            pltpu.VMEM((width, cut), bf16),
            pltpu.VMEM((width, cut), bf16),
            dma((2,)),
            dma((3,)), dma((3,)),
            dma((2, 2, HALF + 1)), dma((2, 2, HALF + 1)),
            dma((2, HALF + 1)), dma((2, HALF + 1)),
            dma((NZ, 3)), dma((NZ, 3)),
            dma((NZ,)), dma((NZ,)),
            dma((NZ,)), dma((NZ,)),
        ],
        compiler_params=pltpu.CompilerParams(collective_id=0, has_side_effects=True, vmem_limit_bytes=48 * 2**20),
    )(tokens, expert_ids, route_logits, expert_gate, expert_up)
    fa = ZA_SCATTER
    fb = width - fa
    part = ROWS // n_dp
    return pl.pallas_call(
        scatter_kernel,
        name="down_scatter",
        out_shape=jax.ShapeDtypeStruct((part, width), bf16),
        in_specs=[vmem, whole],
        out_specs=vmem,
        scratch_shapes=[
            pltpu.VMEM((cut, width), bf16),
            pltpu.VMEM((NZ, NX, ROWS, width), bf16),
            pltpu.VMEM((NZ, NX, ROWS, width), bf16),
            pltpu.VMEM((NZ, NX, ROWS, width), bf16),
            pltpu.VMEM((2, 2, HALF + 1, 2, ROWS, fa), bf16),
            pltpu.VMEM((2, 2, HALF + 1, 2, ROWS, fa), bf16),
            pltpu.VMEM((2, HALF + 1, ROWS, fb), bf16),
            pltpu.VMEM((2, HALF + 1, ROWS, fb), bf16),
            pltpu.VMEM((NZ, 3, ROWS, fb), bf16),
            pltpu.VMEM((NZ, 3, ROWS, fb), bf16),
            pltpu.VMEM((3, ROWS, fa), bf16),
            pltpu.VMEM((3, ROWS, fa), bf16),
            pltpu.VMEM((n_dp, part, width), f32),
            pltpu.VMEM((n_dp, part, width), f32),
            dma,
            dma((NZ,)), dma((NZ,)),
            dma((2, 2, HALF + 1)), dma((2, 2, HALF + 1)),
            dma((2, HALF + 1)), dma((2, HALF + 1)),
            dma((NZ, 3)), dma((NZ, 3)),
            dma((3,)), dma((3,)),
            dma((n_dp,)), dma((n_dp,)),
        ],
        compiler_params=pltpu.CompilerParams(collective_id=1, has_side_effects=True, vmem_limit_bytes=60 * 2**20),
    )(hidden, expert_down)


def solution(mesh):
    placed = (
        P("ep", None),
        P("ep", None),
        P("ep", None),
        P("ep", None, "dp"),
        P("ep", None, "dp"),
        P("ep", "dp", None),
    )
    return jax.shard_map(
        on_device, mesh=mesh, in_specs=placed, out_specs=P(("ep", "dp"), None), check_vma=False
    )
```

time: 403 us -> 145 us (0.36)
  the two profiles are of different devices: /device:TPU:1 before, /device:TPU:6 now
where the time goes in v1:
time: 145 us; the launch traced here: 144 us
  Pallas kernels  137 us (94%)
  local copies, waits for them, and re-layouts  7.74 us (5%)
    pallas_call x1, Pallas kernels, on_device(): pl.pallas_call(gather_kernel, name='gather_up', out_shape=jax.ShapeDtypeS...  68.6 us
    pallas_call x1, Pallas kernels, on_device(): pl.pallas_call(scatter_kernel, name='down_scatter', out_shape=jax.ShapeDt...  68.1 us
    unnamed x11, local copies, waits for them, and re-layouts  7.74 us

profile of v1, /device:TPU:6, one launch (start us, length us, event | category | flops | bytes accessed | tf_op | source)
XLA Modules:
  0.0 144.5 jit_solution(4899571035080158452)
XLA Ops:
  0.0 0.8 copy.7.ids
  0.8 0.8 copy.8.logits
  1.5 0.0 copy-start.1
  1.5 1.5 %copy-done.1 = bf16[1,3584,256]{2,1,0:T(8,128)(2,1)S(1)} copy-done((bf16[1,3584,256]{2,1,0:T(8,128)(2,1)S(1)}, bf16[1,3584,256]{2,1,0:T(8,128)(2,1)}, u32[]{:S(2)}) %copy-start.1) | copy-done | bytes 1835032
  3.0 0.0 copy-start.2
  3.0 1.5 %copy-done.2 = bf16[1,3584,256]{2,1,0:T(8,128)(2,1)S(1)} copy-done((bf16[1,3584,256]{2,1,0:T(8,128)(2,1)S(1)}, bf16[1,3584,256]{2,1,0:T(8,128)(2,1)}, u32[]{:S(2)}) %copy-start.2) | copy-done | bytes 1835032
  4.5 0.0 copy-start.3
  4.5 0.9 copy-done.3
  5.4 68.6 %gather_up.1.hid = bf16[16,2,4,16,256]{4,3,2,1,0:T(8,128)(2,1)S(1)} custom-call(bf16[16,3584]{1,0:T(8,128)(2,1)S(1)} %copy-done.3, s32[16,8]{1,0:T(8,128)S(1)} %copy.7.ids, f32[16,8]{1,0:T(8,128)S(1)} %copy.8.logits, bf16[1,3584,256]{2,1,0:T(8,128)(2,1)S(1)} %copy-done.1, bf16[1,3584,256]{2,1,0:T(8,128)(2,1)S(1)} %copy-done.2), custom_call_target="tpu_custom_call" | custom-call | tf_op jit(solution)/shard_map/gather_up/pallas_call | solution.py:468
  74.0 0.0 copy-start
  74.0 1.0 copy-done
  75.0 68.1 %down_scatter.1 = bf16[4,3584]{1,0:T(4,128)(2,1)} custom-call(bf16[16,2,4,16,256]{4,3,2,1,0:T(8,128)(2,1)} %copy-done, bf16[1,256,3584]{2,1,0:T(8,128)(2,1)} %wd_hbm.1), custom_call_target="tpu_custom_call" | custom-call | tf_op jit(solution)/shard_map/down_scatter/pallas_call | solution.py:492
  143.1 1.4 copy.10
Async XLA Ops:
  1.5 1.5 %copy-start.1 = (bf16[1,3584,256]{2,1,0:T(8,128)(2,1)S(1)}, bf16[1,3584,256]{2,1,0:T(8,128)(2,1)}, u32[]{:S(2)}) copy-start(bf16[1,3584,256]{2,1,0:T(8,128)(2,1)} %wg_hbm.1) | copy-start | bytes 5505028
  3.0 1.5 %copy-start.2 = (bf16[1,3584,256]{2,1,0:T(8,128)(2,1)S(1)}, bf16[1,3584,256]{2,1,0:T(8,128)(2,1)}, u32[]{:S(2)}) copy-start(bf16[1,3584,256]{2,1,0:T(8,128)(2,1)} %wu_hbm.1) | copy-start | bytes 5505028
  4.5 0.9 copy-start.3
  74.0 1.0 copy-start
